TPU v7x, 256 devices: a whole 4x4x8 slice. The times are simulated.
256 devices in a mesh: row: 16 (over y_lo, z), col: 16 (over x, y_hi, core).
Axes of the slice: x: 4, y: 4 (y_hi: 2, y_lo: 2; y = y_hi * 2 + y_lo), z: 8, core: 2. Of those that a mesh axis runs over, the one named last changes fastest.
Arguments:
- field: float32 [512, 64, 8, 512], P('row', 'col'), may hold values from -6 to 6
- modes: int32 [3, 256], replicated, may hold values from 0 to 511, as said below
Outputs:
- spectrum: float32 [64, 512, 8, 512], P(None, 'col', None, 'row')
- localized: float32 [512, 512], replicated
Inputs may be any that keep to these rules, and one draw needn't show every extreme that they name: `modes`: row 0 holds kx in 0 to 255, row 1 ky in 0 to 511, row 2 kz in 0 to 63; triples may repeat.
All inputs are finite; a program needn't handle non-finite values.
Results may differ from a plain program's by a relative error of at most 0.00013.
Values sent between devices are 32-bit elements; how exact they have to be, the bound alone decides.
A program may use at most 128 MiB of HBM per device.

v0:
```python
import functools
import math

import jax
import jax.numpy as jnp
import numpy as np
from jax import lax
from jax.experimental import pallas as pl
from jax.experimental.pallas import tpu as pltpu
from jax.sharding import PartitionSpec as P

NX, NY, NZ, MEMBERS, MODES, REACH = 512, 512, 64, 8, 256, 64
PEERS = 16
LEVELS = NZ // PEERS
ROWS = NY // PEERS
CHUNKS = 8
AHEAD = 3
F32, BF16 = jnp.float32, jnp.bfloat16
MESH = pl.DeviceIdType.MESH
NT = (((1,), (1,)), ((), ()))
NN = (((1,), (0,)), ((), ()))


def halves(table):
    high = table.astype(jnp.bfloat16)
    low = (table - high.astype(np.float32)).astype(jnp.bfloat16)
    return np.stack([high, low])


@functools.cache
def x_table():
    half, block, part, wave = np.meshgrid(np.arange(2), np.arange(16), np.arange(2), np.arange(8), indexing="ij")
    kx = (block * 16 + half * 8 + wave).reshape(-1)
    part = part.reshape(-1)
    angle = 2 * np.pi * (kx[:, None] * np.arange(NX)[None, :] % NX) / NX
    table = np.where(part[:, None] == 0, np.cos(angle), -np.sin(angle)) / math.sqrt(NX * NY * NZ)
    return halves(table.astype(np.float32))


@functools.cache
def y_table():
    peer, out_part, low, out_member = np.meshgrid(np.arange(16), np.arange(2), np.arange(2), np.arange(8), indexing="ij")
    k2 = (peer * 2 + low).reshape(-1)[:, None]
    out_part, out_member = out_part.reshape(-1)[:, None], out_member.reshape(-1)[:, None]
    part, cell, member = np.meshgrid(np.arange(2), np.arange(32), np.arange(8), indexing="ij")
    part, cell, member = (a.reshape(-1)[None, :] for a in (part, cell, member))
    angle = 2 * np.pi * (cell * k2 % 32) / 32
    same = np.cos(angle)
    cross = np.where(out_part == 0, np.sin(angle), -np.sin(angle))
    table = np.where(out_part == part, same, cross) * (member == out_member)
    return halves(table.astype(np.float32))


@functools.cache
def y_twiddle():
    k1 = np.arange(16)[:, None]
    cell = (np.arange(256) // 8)[None, :]
    angle = 2 * np.pi * k1 * cell / NY
    return np.stack([np.cos(angle), np.sin(angle)], axis=1).reshape(32, 256).astype(np.float32)


@functools.cache
def lane_order():
    half, part, k1, wave = np.meshgrid(np.arange(2), np.arange(2), np.arange(16), np.arange(8), indexing="ij")
    target = (k1 * 32 + half * 16 + wave * 2 + part).reshape(-1)
    return (target[:, None] == np.arange(512)[None, :]).astype(jnp.bfloat16)


@functools.cache
def spread():
    part, cell, _ = np.meshgrid(np.arange(2), np.arange(32), np.arange(8), indexing="ij")
    source = (part * 32 + cell).reshape(-1)
    return (np.arange(128)[:, None] == source[None, :]).astype(jnp.bfloat16)


def quarter(a, b, c, d):
    (ar, ai), (br, bi), (cr, ci), (dr, di) = a, b, c, d
    s0r, s0i, s1r, s1i = ar + cr, ai + ci, ar - cr, ai - ci
    s2r, s2i, s3r, s3i = br + dr, bi + di, br - dr, bi - di
    return (
        (s0r + s2r, s0i + s2i),
        (s1r + s3i, s1i - s3r),
        (s0r - s2r, s0i - s2i),
        (s1r - s3i, s1i + s3r),
    )


def turn(value, numerator, denominator):
    re, im = value
    step = numerator % denominator
    if step == 0:
        return value
    if 4 * step == denominator:
        return (im, -re)
    if 8 * step == denominator:
        root = math.sqrt(0.5)
        return ((re + im) * root, (im - re) * root)
    if 8 * step == 3 * denominator:
        root = math.sqrt(0.5)
        return ((im - re) * root, -(re + im) * root)
    c = math.cos(2 * math.pi * step / denominator)
    s = math.sin(2 * math.pi * step / denominator)
    return (re * c + im * s, im * c - re * s)


def transform16(values):
    inner = [quarter(values[n], values[4 + n], values[8 + n], values[12 + n]) for n in range(4)]
    out = [None] * 16
    for k1 in range(4):
        column = [turn(inner[n][k1], n * k1, 16) for n in range(4)]
        for k2, value in enumerate(quarter(*column)):
            out[k1 + 4 * k2] = value
    return out


def split(value):
    high = value.astype(BF16)
    return high, (value - high.astype(F32)).astype(BF16)


def dot(a, b, dims):
    return lax.dot_general(a, b, dims, preferred_element_type=F32)


def cosine_of_turns(steps, period):
    turns = steps * (1.0 / period)
    turns = turns - jnp.floor(turns)
    s = (0.25 - jnp.abs(turns - 0.5)) * (2.0 * math.pi)
    s2 = s * s
    poly = 1.0 / 6227020800.0
    for c in (-1.0 / 39916800.0, 1.0 / 362880.0, -1.0 / 5040.0, 1.0 / 120.0, -1.0 / 6.0, 1.0):
        poly = poly * s2 + c
    return -(poly * s)


def exchange_kernel(
    field, modes, x_tab, y_tab, y_twid, spread_tab,
    levels_out, local_out,
    cells, x_t, y_t, tw, spr, cells_parts, lines, blocks, y_parts, waves,
    coef_one, coef_mine, coef_col, coef_row, coef_sum, coef_all, local_buf,
    load_sem, table_sem, row_send, row_recv, col_send, col_recv, own_sem,
    small_send, small_recv, local_sem,
):
    row, col = lax.axis_index("row"), lax.axis_index("col")
    z_at, y_lo = lax.rem(row, 8), row // 8

    def row_peer(k):
        return lax.rem(z_at + k, 8) + 8 * lax.rem(y_lo + k // 8, 2)

    def col_peer(k):
        return lax.rem(col + k, PEERS)

    barrier = pltpu.get_barrier_semaphore()

    @pl.loop(1, PEERS)
    def _(k):
        pl.semaphore_signal(barrier, inc=1, device_id={"row": row_peer(k)}, device_id_type=MESH)
        pl.semaphore_signal(barrier, inc=1, device_id={"col": col_peer(k)}, device_id_type=MESH)

    def load(level):
        return pltpu.make_async_copy(field.at[:, level], cells.at[level], load_sem.at[level])

    tables = [
        pltpu.make_async_copy(source, target, table_sem.at[i])
        for i, (source, target) in enumerate(((x_tab, x_t), (y_tab, y_t), (y_twid, tw), (spread_tab, spr)))
    ]
    tables[0].start()
    for level in range(LEVELS):
        load(level).start()
    for table in tables[1:]:
        table.start()

    def row_copy(chunk, k):
        peer = row_peer(k)
        return pltpu.make_async_remote_copy(
            src_ref=lines.at[chunk, peer], dst_ref=blocks.at[chunk, row],
            send_sem=row_send.at[chunk], recv_sem=row_recv.at[chunk],
            device_id={"row": peer}, device_id_type=MESH,
        )

    def col_copy(chunk, k):
        peer = col_peer(k)
        return pltpu.make_async_remote_copy(
            src_ref=waves.at[chunk, peer], dst_ref=levels_out.at[chunk, col],
            send_sem=col_send.at[chunk], recv_sem=col_recv.at[chunk],
            device_id={"col": peer}, device_id_type=MESH,
        )

    def own_copy(chunk):
        return pltpu.make_async_copy(waves.at[chunk, col], levels_out.at[chunk, col], own_sem.at[chunk])

    def wait_bytes(ref, sem):
        pltpu.make_async_copy(ref, ref, sem).wait()

    def send_rows(chunk):
        @pl.loop(1, PEERS)
        def _(k):
            row_copy(chunk, k).start()

    def x_transform(level, half):
        chunk = level * 2 + half
        table = pl.ds(half * 256, 256)
        high, low = cells_parts[0], cells_parts[1]
        value = dot(x_t[0, table], high, NT) + dot(x_t[0, table], low, NT) + dot(x_t[1, table], high, NT)
        lines[chunk] = value.reshape(PEERS, 16, 256)
        blocks[chunk, row] = lines[chunk, row]

    tables[0].wait()
    for level in range(LEVELS):
        load(level).wait()
        high, low = split(cells[level].reshape(256, NX))
        cells_parts[0], cells_parts[1] = high, low
        for half in range(2):
            x_transform(level, half)
            if level == 0 and half == 0:
                pl.semaphore_wait(barrier, 2 * (PEERS - 1))
            if level * 2 + half < AHEAD:
                send_rows(level * 2 + half)
    for table in tables[1:]:
        table.wait()

    def mode_row(i):
        return modes[i : i + 1, :].astype(F32)

    def down(value):
        return jnp.broadcast_to(value, (128, MODES)).T

    kx = mode_row(0)
    block = jnp.floor(kx * (1.0 / 16.0))
    half = jnp.floor((kx - 16.0 * block) * 0.125)
    place = half * 256.0 + block * 16.0 + (kx - 16.0 * block - 8.0 * half)
    place = down(place)
    lane = lax.broadcasted_iota(jnp.int32, (MODES, 128), 1)
    lane_f = lane.astype(F32)
    choose = jnp.concatenate(
        [
            jnp.concatenate([(place + 8.0 * part == lane_f + 128.0 * t).astype(F32) for t in range(4)], axis=1)
            for part in range(2)
        ],
        axis=0,
    ).astype(BF16)
    cell = lax.rem(lane, 32).astype(F32) + (row * ROWS).astype(F32)
    steps = down(mode_row(1)) * cell - jnp.where(lane >= 32, 128.0, 0.0)
    phase_high, phase_low = split(cosine_of_turns(steps, float(NY)))
    phase = dot(phase_high, spr[...], NN) + dot(phase_low, spr[...], NN)
    cos_y, sin_y = phase[:, :256], phase[:, 256:]
    level_row = lax.broadcasted_iota(jnp.int32, (8, MODES), 0)
    z_cell = lax.rem(level_row, 4).astype(F32) + (col * LEVELS).astype(F32)
    z_steps = mode_row(2) * z_cell - jnp.where(level_row >= 4, 16.0, 0.0)
    z_phase = cosine_of_turns(z_steps, float(NZ))
    gather_member = (
        lax.rem(lax.broadcasted_iota(jnp.int32, (8, 256), 1), 8) == lax.broadcasted_iota(jnp.int32, (8, 256), 0)
    ).astype(F32).astype(BF16)
    coef_re = jnp.zeros((8, MODES), F32)
    coef_im = jnp.zeros((8, MODES), F32)
    for level in range(LEVELS):
        high, low = split(lines[2 * level : 2 * level + 2].reshape(512, 256))
        at_modes = dot(choose, high, NN) + dot(choose, low, NN)
        re, im = at_modes[:MODES], at_modes[MODES:]
        out_re = re * cos_y + im * sin_y
        out_im = im * cos_y - re * sin_y
        sums = []
        for value in (out_re, out_im):
            high, low = split(value)
            sums.append(dot(gather_member, high, NT) + dot(gather_member, low, NT))
        c, s = z_phase[level : level + 1], z_phase[4 + level : 5 + level]
        coef_re += sums[0] * c + sums[1] * s
        coef_im += sums[1] * c - sums[0] * s
    for t in range(2):
        coef_one[t] = coef_re[:, 128 * t : 128 * t + 128]
        coef_one[2 + t] = coef_im[:, 128 * t : 128 * t + 128]

    def tile_copy(k):
        peer = col_peer(k)
        return pltpu.make_async_remote_copy(
            src_ref=coef_one.at[lax.rem(peer, 4)], dst_ref=coef_col.at[col],
            send_sem=small_send.at[0], recv_sem=small_recv.at[0], device_id={"col": peer}, device_id_type=MESH,
        )

    def sum_copy(k):
        return pltpu.make_async_remote_copy(
            src_ref=coef_mine, dst_ref=coef_row.at[row],
            send_sem=small_send.at[1], recv_sem=small_recv.at[1], device_id={"row": row_peer(k)}, device_id_type=MESH,
        )

    def share_copy(k):
        peer = (col // 4) * 4 + lax.rem(col + k, 4)
        return pltpu.make_async_remote_copy(
            src_ref=coef_sum, dst_ref=coef_all.at[lax.rem(col, 4)],
            send_sem=small_send.at[2], recv_sem=small_recv.at[2], device_id={"col": peer}, device_id_type=MESH,
        )

    def start_all(copy, count):
        @pl.loop(1, count)
        def _(k):
            copy(k).start()

    coef_col[col] = coef_one[lax.rem(col, 4)]
    start_all(tile_copy, PEERS)

    def small_step(step):
        if step == 0:
            wait_bytes(coef_col.at[pl.ds(0, PEERS - 1)], small_recv.at[0])
            total = coef_col[0]
            for i in range(1, PEERS):
                total = total + coef_col[i]
            coef_mine[...] = total
            coef_row[row] = total
            start_all(sum_copy, PEERS)
        elif step == 1:
            wait_bytes(coef_row.at[pl.ds(0, PEERS - 1)], small_recv.at[1])
            total = coef_row[0]
            for i in range(1, PEERS):
                total = total + coef_row[i]
            coef_sum[...] = total
            coef_all[lax.rem(col, 4)] = total
            start_all(share_copy, 4)
        else:
            wait_bytes(coef_all.at[pl.ds(0, 3)], small_recv.at[2])
            coef = jnp.concatenate([coef_all[i] for i in range(4)], axis=1)
            anomaly = coef - jnp.mean(coef, axis=0, keepdims=True)
            turned = anomaly.T
            a_high, a_low = split(turned)
            b_high, b_low = split(anomaly)
            kx, ky, kz = mode_row(0), mode_row(1), mode_row(2)
            ky = jnp.where(ky < NY // 2, ky, ky - NY)
            kz = jnp.where(kz < NZ // 2, kz, kz - NZ)
            dist = jnp.zeros((MODES, MODES), F32)
            for wave in (kx, ky, kz):
                tall = down(wave)
                tall = jnp.concatenate([tall, tall], axis=1)
                dist += (tall - wave) ** 2
            taper = jnp.exp(-dist * (1.0 / (2.0 * REACH * REACH))) * (1.0 / (MEMBERS - 1))
            for i in range(2):
                at = slice(i * MODES, (i + 1) * MODES)
                cov = dot(a_high[at], b_high, NN) + dot(a_high[at], b_low, NN) + dot(a_low[at], b_high, NN)
                local_buf[at, :MODES] = cov[:, :MODES] * taper
                local_buf[at, MODES:] = cov[:, MODES:] * taper
            pltpu.make_async_copy(local_buf, local_out, local_sem).start()

    @pl.loop(0, CHUNKS)
    def _(chunk):
        @pl.when(chunk + AHEAD < CHUNKS)
        def _():
            send_rows(chunk + AHEAD)

        wait_bytes(blocks.at[chunk, pl.ds(0, PEERS - 1)], row_recv.at[chunk])
        for t in range(2):
            lanes = pl.ds(t * 128, 128)
            values = [(blocks[chunk, i, 0:8, lanes], blocks[chunk, i, 8:16, lanes]) for i in range(16)]
            out = transform16(values)
            for pair in range(8):
                parts = []
                for k1 in (2 * pair, 2 * pair + 1):
                    re, im = out[k1]
                    if k1 > 0:
                        c = tw[2 * k1 : 2 * k1 + 1, lanes]
                        s = tw[2 * k1 + 1 : 2 * k1 + 2, lanes]
                        re, im = re * c + im * s, im * c - re * s
                    parts.append((re, im))
                for part in range(2):
                    value = jnp.concatenate([parts[0][part], parts[1][part]], axis=0)
                    high, low = split(value)
                    at = pl.ds(part * 256 + t * 128, 128)
                    y_parts[pl.ds(16 * pair, 16), at] = high
                    y_parts[pl.ds(128 + 16 * pair, 16), at] = low
        both = dot(y_t[0], y_parts[...], NT)
        value = both[:, :128] + both[:, 128:] + dot(y_t[1], y_parts[pl.ds(0, 128)], NT)
        waves[chunk] = value.reshape(PEERS, 32, 128)

        @pl.loop(1, PEERS)
        def _(k):
            col_copy(chunk, k).start()

        own_copy(chunk).start()

        for step, at in enumerate((1, 3, 5)):
            @pl.when(chunk == at)
            def _(step=step):
                small_step(step)

    pltpu.make_async_copy(local_buf, local_out, local_sem).wait()
    wait_bytes(coef_col.at[pl.ds(0, PEERS - 1)], small_send.at[0])
    wait_bytes(coef_row.at[pl.ds(0, PEERS - 1)], small_send.at[1])
    wait_bytes(coef_all.at[pl.ds(0, 3)], small_send.at[2])

    @pl.loop(0, CHUNKS)
    def _(chunk):
        wait_bytes(lines.at[chunk, pl.ds(0, PEERS - 1)], row_send.at[chunk])
        wait_bytes(waves.at[chunk, pl.ds(0, PEERS - 1)], col_send.at[chunk])
        own_copy(chunk).wait()
        wait_bytes(levels_out.at[chunk, pl.ds(0, PEERS - 1)], col_recv.at[chunk])


def exchange(field, modes):
    any_space = pl.BlockSpec(memory_space=pl.ANY)
    dma = pltpu.SemaphoreType.DMA
    return pl.pallas_call(
        exchange_kernel,
        out_shape=(
            jax.ShapeDtypeStruct((CHUNKS, PEERS, 32, 128), F32),
            jax.ShapeDtypeStruct((2 * MODES, 2 * MODES), F32),
        ),
        in_specs=[any_space, pl.BlockSpec(memory_space=pltpu.VMEM)] + [any_space] * 4,
        out_specs=(any_space, any_space),
        scratch_shapes=[
            pltpu.VMEM((LEVELS, ROWS, MEMBERS, NX), F32),
            pltpu.VMEM((2, 512, 512), BF16),
            pltpu.VMEM((2, 512, 512), BF16),
            pltpu.VMEM((32, 256), F32),
            pltpu.VMEM((128, 512), BF16),
            pltpu.VMEM((2, 256, NX), BF16),
            pltpu.VMEM((CHUNKS, PEERS, 16, 256), F32),
            pltpu.VMEM((CHUNKS, PEERS, 16, 256), F32),
            pltpu.VMEM((256, 512), BF16),
            pltpu.VMEM((CHUNKS, PEERS, 32, 128), F32),
            pltpu.VMEM((4, 8, 128), F32),
            pltpu.VMEM((8, 128), F32),
            pltpu.VMEM((PEERS, 8, 128), F32),
            pltpu.VMEM((PEERS, 8, 128), F32),
            pltpu.VMEM((8, 128), F32),
            pltpu.VMEM((4, 8, 128), F32),
            pltpu.VMEM((512, 512), F32),
            dma((LEVELS,)),
            dma((4,)),
            dma((CHUNKS,)),
            dma((CHUNKS,)),
            dma((CHUNKS,)),
            dma((CHUNKS,)),
            dma((CHUNKS,)),
            dma((3,)),
            dma((3,)),
            dma,
        ],
        compiler_params=pltpu.CompilerParams(collective_id=0, has_side_effects=True, vmem_limit_bytes=48 << 20),
        cost_estimate=pl.CostEstimate(flops=10**10, bytes_accessed=8 << 20, transcendentals=0),
        name="exchange",
    )(field, modes, x_table(), y_table(), y_twiddle(), spread())


def levels_kernel(levels, order, local_in, spectrum, local, inner, rows):
    group = pl.program_id(1)

    @pl.when(group == 0)
    def _():
        for level in range(LEVELS):
            for half in range(2):
                values = [
                    (levels[2 * level + half, i, 0, 0], levels[2 * level + half, i, 1, 0]) for i in range(PEERS)
                ]
                for a, value in enumerate(transform16(values)):
                    value = turn(value, level * a, NZ)
                    for part in range(2):
                        inner[half, part, level, a] = value[part]

    for i in range(4):
        a = group * 4 + i
        for half in range(2):
            values = [(inner[half, 0, n, a], inner[half, 1, n, a]) for n in range(LEVELS)]
            for b, value in enumerate(quarter(*values)):
                for part in range(2):
                    at = pl.ds((half * 2 + part) * 128, 128)
                    rows[pl.ds((b * 4 + i) * 8, 8), at] = value[part]
    high, low = split(rows[...])
    value = dot(high, order[...], NN) + dot(low, order[...], NN)
    for b in range(4):
        for i in range(4):
            for k1 in range(16):
                at = (b * 4 + i) * 8
                spectrum[b, i, k1] = value[at : at + 8, 32 * k1 : 32 * k1 + 32]
    local[...] = local_in[...]


def from_levels(levels, local):
    levels = levels.reshape(CHUNKS, PEERS, 2, 2, 8, 128)
    block = 2 * MODES // 8
    spectrum, local = pl.pallas_call(
        levels_kernel,
        grid=(2, 4),
        out_shape=(
            jax.ShapeDtypeStruct((4, 16, 32, 8, 32), F32),
            jax.ShapeDtypeStruct((2 * MODES, 2 * MODES), F32),
        ),
        in_specs=[
            pl.BlockSpec((CHUNKS, PEERS, 2, 1, 8, 128), lambda low, group: (0, 0, 0, low, 0, 0)),
            pl.BlockSpec((512, 512), lambda low, group: (0, 0)),
            pl.BlockSpec((block, 2 * MODES), lambda low, group: (low * 4 + group, 0)),
        ],
        out_specs=(
            pl.BlockSpec((4, 4, 16, 8, 32), lambda low, group: (0, group, low, 0, 0)),
            pl.BlockSpec((block, 2 * MODES), lambda low, group: (low * 4 + group, 0)),
        ),
        scratch_shapes=[
            pltpu.VMEM((2, 2, LEVELS, 16, 8, 128), F32),
            pltpu.VMEM((128, 512), F32),
        ],
        compiler_params=pltpu.CompilerParams(vmem_limit_bytes=32 << 20),
        cost_estimate=pl.CostEstimate(flops=10**9, bytes_accessed=10 << 20, transcendentals=0),
        name="from_levels",
    )(levels, lane_order(), local)
    return spectrum.reshape(NZ, NY // PEERS, MEMBERS, 2 * NX // 32), local


def per_device(field, modes):
    levels, local = exchange(field, modes)
    return from_levels(levels, local)


def solution(mesh):
    return jax.shard_map(
        per_device,
        mesh=mesh,
        in_specs=(P("row", "col", None, None), P()),
        out_specs=(P(None, "col", None, "row"), P()),
        check_vma=False,
    )
```

profile of v0, /device:TPU:1, one launch (start us, length us, event | category | flops | bytes accessed | tf_op | source)
XLA Modules:
  0.0 89.9 jit_solution(12553601904327629280)
XLA Ops:
  0.6 0.0 copy-start.1
  0.6 0.7 copy-done.1
  1.3 0.0 copy-start.2
  1.3 1.2 %copy-done.2 = bf16[2,512,512]{2,1,0:T(8,128)(2,1)S(1)} copy-done((bf16[2,512,512]{2,1,0:T(8,128)(2,1)S(1)}, bf16[2,512,512]{2,1,0:T(8,128)(2,1)}, u32[]{:S(2)}) %copy-start.2) | copy-done | bytes 1048600
  2.5 0.0 copy-start.3
  2.5 1.2 %copy-done.3 = bf16[2,512,512]{2,1,0:T(8,128)(2,1)S(1)} copy-done((bf16[2,512,512]{2,1,0:T(8,128)(2,1)S(1)}, bf16[2,512,512]{2,1,0:T(8,128)(2,1)}, u32[]{:S(2)}) %copy-start.3) | copy-done | bytes 1048600
  3.8 0.0 copy-start.5
  3.8 0.9 %copy-done.5 = bf16[128,512]{1,0:T(8,128)(2,1)S(1)} copy-done((bf16[128,512]{1,0:T(8,128)(2,1)S(1)}, bf16[128,512]{1,0:T(8,128)(2,1)}, u32[]{:S(2)}) %copy-start.5) | copy-done | bytes 131096
  4.7 0.0 copy-start.6
  4.7 0.8 copy-done.6
  5.4 0.0 copy-start.4
  5.4 66.9 %exchange.1 = (f32[8,16,32,128]{3,2,1,0:T(8,128)S(1)}, f32[512,512]{1,0:T(8,128)S(1)}) custom-call(f32[32,4,8,512]{3,2,1,0:T(8,128)} %field.1, s32[3,256]{1,0:T(4,128)S(1)} %copy-done.1, bf16[2,512,512]{2,1,0:T(8,128)(2,1)S(1)} %copy-done.3, bf16[2,512,512]{2,1,0:T(8,128)(2,1)S(1)} %copy-done.2, f32[32,256]{1,0:T(8,128)S(1)} %copy-done.6, ...), custom_call_target="tpu_custom_call" | custom-call | flops 10000000000 | bytes 8388608 | tf_op jit(solution)/shard_map/exchange/pallas_call | solution.py:398
  72.4 0.0 copy-done.4
  72.4 6.5 %from_levels.1 = (f32[4,16,32,8,32]{4,3,2,1,0:T(8,128)S(1)}, f32[512,512]{1,0:T(8,128)}) custom-call(f32[8,16,2,2,8,128]{5,4,3,2,1,0:T(8,128)S(1)} %bitcast.3, bf16[512,512]{1,0:T(8,128)(2,1)S(1)} %copy-done.4, f32[512,512]{1,0:T(8,128)S(1)} %get-tuple-element.7.local_in), custom_call_target="tpu_custom_call" | custom-call | flops 1000000000 | bytes 10485760 | tf_op jit(solution)/shard_map/from_levels/pallas_call | solution.py:477
  78.9 0.0 copy-start
  78.9 3.2 %copy-done = f32[4,16,32,8,32]{4,3,2,1,0:T(8,128)} copy-done((f32[4,16,32,8,32]{4,3,2,1,0:T(8,128)}, f32[4,16,32,8,32]{4,3,2,1,0:T(8,128)S(1)}, u32[]{:S(2)}) %copy-start) | copy-done | bytes 2097176
  82.2 7.8 %copy.9 = f32[64,32,8,32]{0,3,2,1:T(8,128)} copy(f32[64,32,8,32]{3,2,1,0:T(8,128)} %bitcast.2) | data formatting | bytes 4194304
Async XLA Ops:
  0.6 0.7 copy-start.1
  1.3 1.2 %copy-start.2 = (bf16[2,512,512]{2,1,0:T(8,128)(2,1)S(1)}, bf16[2,512,512]{2,1,0:T(8,128)(2,1)}, u32[]{:S(2)}) copy-start(bf16[2,512,512]{2,1,0:T(8,128)(2,1)} %constant.11.clone.y_tab) | copy-start | bytes 3145732
  2.5 1.2 %copy-start.3 = (bf16[2,512,512]{2,1,0:T(8,128)(2,1)S(1)}, bf16[2,512,512]{2,1,0:T(8,128)(2,1)}, u32[]{:S(2)}) copy-start(bf16[2,512,512]{2,1,0:T(8,128)(2,1)} %constant.10.clone.x_tab) | copy-start | bytes 3145732
  3.8 0.9 %copy-start.5 = (bf16[128,512]{1,0:T(8,128)(2,1)S(1)}, bf16[128,512]{1,0:T(8,128)(2,1)}, u32[]{:S(2)}) copy-start(bf16[128,512]{1,0:T(8,128)(2,1)} %constant.13.clone.spread_tab) | copy-start | bytes 393220
  4.7 0.8 copy-start.6
  5.4 67.0 %copy-start.4 = (bf16[512,512]{1,0:T(8,128)(2,1)S(1)}, bf16[512,512]{1,0:T(8,128)(2,1)}, u32[]{:S(2)}) copy-start(bf16[512,512]{1,0:T(8,128)(2,1)} %constant.14.clone.order) | copy-start | bytes 1572868
  78.9 3.2 %copy-start = (f32[4,16,32,8,32]{4,3,2,1,0:T(8,128)}, f32[4,16,32,8,32]{4,3,2,1,0:T(8,128)S(1)}, u32[]{:S(2)}) copy-start(f32[4,16,32,8,32]{4,3,2,1,0:T(8,128)S(1)} %get-tuple-element.8) | copy-start | bytes 6291460
where the time goes:
time: 90.3 us; the launch traced here: 89.9 us
  Pallas kernels  73.5 us (81%)
  local copies, waits for them, and re-layouts  15.8 us (17%)
    pallas_call x1, Pallas kernels, exchange(): pl.pallas_call(exchange_kernel, out_shape=(jax.ShapeDtypeStruct((CHUNKS,...  66.9 us
    unnamed x15, local copies, waits for them, and re-layouts  15.8 us
    pallas_call x1, Pallas kernels, from_levels(): pl.pallas_call(levels_kernel, grid=(2, 4), out_shape=(jax.ShapeDtypeStruc...  6.53 us

commit v1 on v0

--- a/solution.py
+++ b/solution.py
@@ -13,8 +13,10 @@
 PEERS = 16
 LEVELS = NZ // PEERS
 ROWS = NY // PEERS
+PAIRS = 4
 CHUNKS = 8
 AHEAD = 3
+VMEM = 67_043_328
 F32, BF16 = jnp.float32, jnp.bfloat16
 MESH = pl.DeviceIdType.MESH
 NT = (((1,), (1,)), ((), ()))
@@ -39,38 +41,34 @@
 
 @functools.cache
 def y_table():
-    peer, out_part, low, out_member = np.meshgrid(np.arange(16), np.arange(2), np.arange(2), np.arange(8), indexing="ij")
-    k2 = (peer * 2 + low).reshape(-1)[:, None]
-    out_part, out_member = out_part.reshape(-1)[:, None], out_member.reshape(-1)[:, None]
-    part, cell, member = np.meshgrid(np.arange(2), np.arange(32), np.arange(8), indexing="ij")
-    part, cell, member = (a.reshape(-1)[None, :] for a in (part, cell, member))
-    angle = 2 * np.pi * (cell * k2 % 32) / 32
-    same = np.cos(angle)
+    rows = np.meshgrid(np.arange(16), np.arange(2), np.arange(2), np.arange(2), np.arange(4), indexing="ij")
+    peer, out_part, low, out_member, out_level = (a.reshape(-1)[:, None] for a in rows)
+    columns = np.meshgrid(np.arange(2), np.arange(2), np.arange(32), np.arange(4), indexing="ij")
+    part, member, cell, level = (a.reshape(-1)[None, :] for a in columns)
+    angle = 2 * np.pi * (cell * (peer * 2 + low) % 32) / 32
     cross = np.where(out_part == 0, np.sin(angle), -np.sin(angle))
-    table = np.where(out_part == part, same, cross) * (member == out_member)
+    table = np.where(out_part == part, np.cos(angle), cross) * (member == out_member) * (level == out_level)
     return halves(table.astype(np.float32))
 
 
 @functools.cache
 def y_twiddle():
     k1 = np.arange(16)[:, None]
-    cell = (np.arange(256) // 8)[None, :]
+    cell = (np.arange(128) // 4)[None, :]
     angle = 2 * np.pi * k1 * cell / NY
-    return np.stack([np.cos(angle), np.sin(angle)], axis=1).reshape(32, 256).astype(np.float32)
+    return np.stack([np.cos(angle), np.sin(angle)], axis=1).reshape(32, 128).astype(np.float32)
 
 
 @functools.cache
-def lane_order():
-    half, part, k1, wave = np.meshgrid(np.arange(2), np.arange(2), np.arange(16), np.arange(8), indexing="ij")
-    target = (k1 * 32 + half * 16 + wave * 2 + part).reshape(-1)
-    return (target[:, None] == np.arange(512)[None, :]).astype(jnp.bfloat16)
-
-
-@functools.cache
-def spread():
-    part, cell, _ = np.meshgrid(np.arange(2), np.arange(32), np.arange(8), indexing="ij")
-    source = (part * 32 + cell).reshape(-1)
-    return (np.arange(128)[:, None] == source[None, :]).astype(jnp.bfloat16)
+def z_table():
+    rows = np.meshgrid(np.arange(16), np.arange(2), np.arange(2), np.arange(4), indexing="ij")
+    peer, part, member, level = (a.reshape(-1)[:, None] for a in rows)
+    columns = np.meshgrid(np.arange(2), np.arange(2), np.arange(64), indexing="ij")
+    out_part, out_member, kz = (a.reshape(-1)[None, :] for a in columns)
+    angle = 2 * np.pi * ((4 * peer + level) * kz % NZ) / NZ
+    cross = np.where(out_part == 0, np.sin(angle), -np.sin(angle))
+    table = np.where(out_part == part, np.cos(angle), cross) * (member == out_member)
+    return halves(table.astype(np.float32))
 
 
 def quarter(a, b, c, d):
@@ -134,11 +132,11 @@
 
 
 def exchange_kernel(
-    field, modes, x_tab, y_tab, y_twid, spread_tab,
+    field, modes_in, x_tab, y_tab, y_twid,
     levels_out, local_out,
-    cells, x_t, y_t, tw, spr, cells_parts, lines, blocks, y_parts, waves,
+    cells, modes, x_t, y_t, tw, cells_parts, lines, blocks, y_parts, waves,
     coef_one, coef_mine, coef_col, coef_row, coef_sum, coef_all, local_buf,
-    load_sem, table_sem, row_send, row_recv, col_send, col_recv, own_sem,
+    load_sem, row_send, row_recv, col_send, col_recv, own_sem,
     small_send, small_recv, local_sem,
 ):
     row, col = lax.axis_index("row"), lax.axis_index("col")
@@ -157,18 +155,12 @@
         pl.semaphore_signal(barrier, inc=1, device_id={"row": row_peer(k)}, device_id_type=MESH)
         pl.semaphore_signal(barrier, inc=1, device_id={"col": col_peer(k)}, device_id_type=MESH)
 
-    def load(level):
-        return pltpu.make_async_copy(field.at[:, level], cells.at[level], load_sem.at[level])
-
-    tables = [
-        pltpu.make_async_copy(source, target, table_sem.at[i])
-        for i, (source, target) in enumerate(((x_tab, x_t), (y_tab, y_t), (y_twid, tw), (spread_tab, spr)))
-    ]
-    tables[0].start()
-    for level in range(LEVELS):
-        load(level).start()
-    for table in tables[1:]:
-        table.start()
+    pieces = [(x_tab, x_t)] + [(field.at[:, pl.ds(128 * t, 128)], cells.at[t]) for t in range(NX // 128)]
+    first_pieces = len(pieces)
+    pieces += [(modes_in, modes), (y_twid, tw), (y_tab, y_t)]
+    loads = [pltpu.make_async_copy(source, target, load_sem.at[i]) for i, (source, target) in enumerate(pieces)]
+    for each in loads:
+        each.start()
 
     def row_copy(chunk, k):
         peer = row_peer(k)
@@ -197,27 +189,27 @@
         def _(k):
             row_copy(chunk, k).start()
 
-    def x_transform(level, half):
-        chunk = level * 2 + half
-        table = pl.ds(half * 256, 256)
-        high, low = cells_parts[0], cells_parts[1]
-        value = dot(x_t[0, table], high, NT) + dot(x_t[0, table], low, NT) + dot(x_t[1, table], high, NT)
-        lines[chunk] = value.reshape(PEERS, 16, 256)
-        blocks[chunk, row] = lines[chunk, row]
-
-    tables[0].wait()
-    for level in range(LEVELS):
-        load(level).wait()
-        high, low = split(cells[level].reshape(256, NX))
-        cells_parts[0], cells_parts[1] = high, low
+    for each in loads[:first_pieces]:
+        each.wait()
+    for pair in range(PAIRS):
+        for i in range(2):
+            for t in range(NX // 128):
+                high, low = split(cells[t, pl.ds(2 * pair + i, ROWS * LEVELS, stride=MEMBERS), :])
+                at = (pl.ds(i * 128, 128), pl.ds(t * 128, 128))
+                cells_parts[(0, *at)], cells_parts[(1, *at)] = high, low
         for half in range(2):
-            x_transform(level, half)
-            if level == 0 and half == 0:
+            chunk = pair * 2 + half
+            table = pl.ds(half * 256, 256)
+            high, low = cells_parts[0], cells_parts[1]
+            value = dot(x_t[0, table], high, NT) + dot(x_t[0, table], low, NT) + dot(x_t[1, table], high, NT)
+            lines[chunk] = value.reshape(PEERS, 16, 256)
+            blocks[chunk, row] = lines[chunk, row]
+            if chunk == 0:
                 pl.semaphore_wait(barrier, 2 * (PEERS - 1))
-            if level * 2 + half < AHEAD:
-                send_rows(level * 2 + half)
-    for table in tables[1:]:
-        table.wait()
+            if chunk < AHEAD:
+                send_rows(chunk)
+    for each in loads[first_pieces:]:
+        each.wait()
 
     def mode_row(i):
         return modes[i : i + 1, :].astype(F32)
@@ -239,33 +231,27 @@
         ],
         axis=0,
     ).astype(BF16)
-    cell = lax.rem(lane, 32).astype(F32) + (row * ROWS).astype(F32)
-    steps = down(mode_row(1)) * cell - jnp.where(lane >= 32, 128.0, 0.0)
-    phase_high, phase_low = split(cosine_of_turns(steps, float(NY)))
-    phase = dot(phase_high, spr[...], NN) + dot(phase_low, spr[...], NN)
-    cos_y, sin_y = phase[:, :256], phase[:, 256:]
-    level_row = lax.broadcasted_iota(jnp.int32, (8, MODES), 0)
-    z_cell = lax.rem(level_row, 4).astype(F32) + (col * LEVELS).astype(F32)
-    z_steps = mode_row(2) * z_cell - jnp.where(level_row >= 4, 16.0, 0.0)
-    z_phase = cosine_of_turns(z_steps, float(NZ))
-    gather_member = (
-        lax.rem(lax.broadcasted_iota(jnp.int32, (8, 256), 1), 8) == lax.broadcasted_iota(jnp.int32, (8, 256), 0)
-    ).astype(F32).astype(BF16)
+    cell = (lane // 4).astype(F32) + (row * ROWS).astype(F32)
+    level = lax.rem(lane, 4).astype(F32) + (col * LEVELS).astype(F32)
+    steps = down(mode_row(1)) * cell + down(mode_row(2)) * level * float(NY // NZ)
+    cos = cosine_of_turns(steps, float(NY))
+    sin = cosine_of_turns(steps - 128.0, float(NY))
+    cos, sin = jnp.concatenate([cos, cos], axis=1), jnp.concatenate([sin, sin], axis=1)
+    lane_member = lax.broadcasted_iota(jnp.int32, (8, 256), 1) // 128
+    member = lax.broadcasted_iota(jnp.int32, (8, 256), 0)
     coef_re = jnp.zeros((8, MODES), F32)
     coef_im = jnp.zeros((8, MODES), F32)
-    for level in range(LEVELS):
-        high, low = split(lines[2 * level : 2 * level + 2].reshape(512, 256))
+    for pair in range(PAIRS):
+        gather_member = (lane_member + 2 * pair == member).astype(F32).astype(BF16)
+        high, low = split(lines[2 * pair : 2 * pair + 2].reshape(512, 256))
         at_modes = dot(choose, high, NN) + dot(choose, low, NN)
         re, im = at_modes[:MODES], at_modes[MODES:]
-        out_re = re * cos_y + im * sin_y
-        out_im = im * cos_y - re * sin_y
         sums = []
-        for value in (out_re, out_im):
+        for value in (re * cos + im * sin, im * cos - re * sin):
             high, low = split(value)
             sums.append(dot(gather_member, high, NT) + dot(gather_member, low, NT))
-        c, s = z_phase[level : level + 1], z_phase[4 + level : 5 + level]
-        coef_re += sums[0] * c + sums[1] * s
-        coef_im += sums[1] * c - sums[0] * s
+        coef_re += sums[0]
+        coef_im += sums[1]
     for t in range(2):
         coef_one[t] = coef_re[:, 128 * t : 128 * t + 128]
         coef_one[2 + t] = coef_im[:, 128 * t : 128 * t + 128]
@@ -354,8 +340,8 @@
                 for k1 in (2 * pair, 2 * pair + 1):
                     re, im = out[k1]
                     if k1 > 0:
-                        c = tw[2 * k1 : 2 * k1 + 1, lanes]
-                        s = tw[2 * k1 + 1 : 2 * k1 + 2, lanes]
+                        c = tw[2 * k1 : 2 * k1 + 1, :]
+                        s = tw[2 * k1 + 1 : 2 * k1 + 2, :]
                         re, im = re * c + im * s, im * c - re * s
                     parts.append((re, im))
                 for part in range(2):
@@ -401,14 +387,14 @@
             jax.ShapeDtypeStruct((CHUNKS, PEERS, 32, 128), F32),
             jax.ShapeDtypeStruct((2 * MODES, 2 * MODES), F32),
         ),
-        in_specs=[any_space, pl.BlockSpec(memory_space=pltpu.VMEM)] + [any_space] * 4,
+        in_specs=[any_space] * 5,
         out_specs=(any_space, any_space),
         scratch_shapes=[
-            pltpu.VMEM((LEVELS, ROWS, MEMBERS, NX), F32),
+            pltpu.VMEM((NX // 128, ROWS * LEVELS * MEMBERS, 128), F32),
+            pltpu.VMEM((3, MODES), jnp.int32),
             pltpu.VMEM((2, 512, 512), BF16),
             pltpu.VMEM((2, 512, 512), BF16),
-            pltpu.VMEM((32, 256), F32),
-            pltpu.VMEM((128, 512), BF16),
+            pltpu.VMEM((32, 128), F32),
             pltpu.VMEM((2, 256, NX), BF16),
             pltpu.VMEM((CHUNKS, PEERS, 16, 256), F32),
             pltpu.VMEM((CHUNKS, PEERS, 16, 256), F32),
@@ -421,8 +407,7 @@
             pltpu.VMEM((8, 128), F32),
             pltpu.VMEM((4, 8, 128), F32),
             pltpu.VMEM((512, 512), F32),
-            dma((LEVELS,)),
-            dma((4,)),
+            dma((8,)),
             dma((CHUNKS,)),
             dma((CHUNKS,)),
             dma((CHUNKS,)),
@@ -432,73 +417,53 @@
             dma((3,)),
             dma,
         ],
-        compiler_params=pltpu.CompilerParams(collective_id=0, has_side_effects=True, vmem_limit_bytes=48 << 20),
+        compiler_params=pltpu.CompilerParams(collective_id=0, has_side_effects=True, vmem_limit_bytes=VMEM),
         cost_estimate=pl.CostEstimate(flops=10**10, bytes_accessed=8 << 20, transcendentals=0),
         name="exchange",
-    )(field, modes, x_table(), y_table(), y_twiddle(), spread())
-
-
-def levels_kernel(levels, order, local_in, spectrum, local, inner, rows):
-    group = pl.program_id(1)
-
-    @pl.when(group == 0)
-    def _():
-        for level in range(LEVELS):
-            for half in range(2):
-                values = [
-                    (levels[2 * level + half, i, 0, 0], levels[2 * level + half, i, 1, 0]) for i in range(PEERS)
-                ]
-                for a, value in enumerate(transform16(values)):
-                    value = turn(value, level * a, NZ)
-                    for part in range(2):
-                        inner[half, part, level, a] = value[part]
-
-    for i in range(4):
-        a = group * 4 + i
-        for half in range(2):
-            values = [(inner[half, 0, n, a], inner[half, 1, n, a]) for n in range(LEVELS)]
-            for b, value in enumerate(quarter(*values)):
+    )(field.reshape(-1, NX), modes, x_table(), y_table(), y_twiddle())
+
+
+def levels_kernel(levels, table, local_in, spectrum, local, rows):
+    for half in range(2):
+        for low_k in range(2):
+            value = levels[half, :, :, low_k].reshape(256, 128).T
+            high, low = split(value)
+            out = dot(high, table[0], NN) + dot(high, table[1], NN) + dot(low, table[0], NN)
+            for k1 in range(16):
                 for part in range(2):
-                    at = pl.ds((half * 2 + part) * 128, 128)
-                    rows[pl.ds((b * 4 + i) * 8, 8), at] = value[part]
-    high, low = split(rows[...])
-    value = dot(high, order[...], NN) + dot(low, order[...], NN)
-    for b in range(4):
-        for i in range(4):
-            for k1 in range(16):
-                at = (b * 4 + i) * 8
-                spectrum[b, i, k1] = value[at : at + 8, 32 * k1 : 32 * k1 + 32]
+                    at = (low_k * 16 + k1) * 32 + 16 * half + part
+                    rows[pl.ds(at, 8, stride=2), :] = out[8 * k1 : 8 * k1 + 8, 128 * part : 128 * part + 128]
+    value = rows[...].reshape(NY // PEERS, 32, 128)
+    for member in range(2):
+        spectrum[:, member] = value[:, :, member * NZ : (member + 1) * NZ]
     local[...] = local_in[...]
 
 
 def from_levels(levels, local):
     levels = levels.reshape(CHUNKS, PEERS, 2, 2, 8, 128)
-    block = 2 * MODES // 8
+    block = 2 * MODES // PAIRS
     spectrum, local = pl.pallas_call(
         levels_kernel,
-        grid=(2, 4),
+        grid=(PAIRS,),
         out_shape=(
-            jax.ShapeDtypeStruct((4, 16, 32, 8, 32), F32),
+            jax.ShapeDtypeStruct((NY // PEERS, MEMBERS, 32, NZ), F32),
             jax.ShapeDtypeStruct((2 * MODES, 2 * MODES), F32),
         ),
         in_specs=[
-            pl.BlockSpec((CHUNKS, PEERS, 2, 1, 8, 128), lambda low, group: (0, 0, 0, low, 0, 0)),
-            pl.BlockSpec((512, 512), lambda low, group: (0, 0)),
-            pl.BlockSpec((block, 2 * MODES), lambda low, group: (low * 4 + group, 0)),
+            pl.BlockSpec((2, PEERS, 2, 2, 8, 128), lambda pair: (pair, 0, 0, 0, 0, 0)),
+            pl.BlockSpec((2, 256, 256), lambda pair: (0, 0, 0)),
+            pl.BlockSpec((block, 2 * MODES), lambda pair: (pair, 0)),
         ],
         out_specs=(
-            pl.BlockSpec((4, 4, 16, 8, 32), lambda low, group: (0, group, low, 0, 0)),
-            pl.BlockSpec((block, 2 * MODES), lambda low, group: (low * 4 + group, 0)),
+            pl.BlockSpec((NY // PEERS, 2, 32, NZ), lambda pair: (0, pair, 0, 0)),
+            pl.BlockSpec((block, 2 * MODES), lambda pair: (pair, 0)),
         ),
-        scratch_shapes=[
-            pltpu.VMEM((2, 2, LEVELS, 16, 8, 128), F32),
-            pltpu.VMEM((128, 512), F32),
-        ],
-        compiler_params=pltpu.CompilerParams(vmem_limit_bytes=32 << 20),
-        cost_estimate=pl.CostEstimate(flops=10**9, bytes_accessed=10 << 20, transcendentals=0),
+        scratch_shapes=[pltpu.VMEM((NY // PEERS * 32, 128), F32)],
+        compiler_params=pltpu.CompilerParams(vmem_limit_bytes=VMEM),
+        cost_estimate=pl.CostEstimate(flops=10**9, bytes_accessed=8 << 20, transcendentals=0),
         name="from_levels",
-    )(levels, lane_order(), local)
-    return spectrum.reshape(NZ, NY // PEERS, MEMBERS, 2 * NX // 32), local
+    )(levels, z_table(), local)
+    return jnp.transpose(spectrum, (3, 0, 1, 2)), local
 
 
 def per_device(field, modes):

time: 90.3 us -> 74.4 us (0.82)
  local copies, waits for them, and re-layouts: 15.8 us -> 0 us
    unnamed x15 -> x0, local copies, waits for them, and re-layouts: 15.8 us -> none
where the time goes in v1:
time: 74.4 us; the launch traced here: 74.3 us
  Pallas kernels  73.6 us (99%)
    pallas_call x1, Pallas kernels, exchange(): pl.pallas_call(exchange_kernel, out_shape=(jax.ShapeDtypeStruct((CHUNKS,...  67.6 us
    pallas_call x1, Pallas kernels, from_levels(): pl.pallas_call(levels_kernel, grid=(PAIRS,), out_shape=(jax.ShapeDtypeStr...  6.03 us

profile of v1, /device:TPU:1, one launch (start us, length us, event | category | flops | bytes accessed | tf_op | source)
XLA Modules:
  0.0 74.3 jit_solution(2793173503724017775)
XLA Ops:
  0.6 67.6 %exchange.1 = (f32[8,16,32,128]{3,2,1,0:T(8,128)}, f32[512,512]{1,0:T(8,128)}) custom-call(f32[1024,512]{1,0:T(8,128)} %bitcast.3, s32[3,256]{1,0:T(4,128)} %modes_in.1, bf16[2,512,512]{2,1,0:T(8,128)(2,1)} %constant.8.clone.x_tab, bf16[2,512,512]{2,1,0:T(8,128)(2,1)} %constant.9.clone.y_tab, f32[32,128]{1,0:T(8,128)} %constant.10.clone.y_twid), custom_call_target="tpu_custom_call" | custom-call | flops 10000000000 | bytes 8388608 | tf_op jit(solution)/shard_map/exchange/pallas_call | solution.py:384
  68.2 6.0 %from_levels.1 = (f32[32,8,32,64]{3,2,1,0:T(8,128)}, f32[512,512]{1,0:T(8,128)}) custom-call(f32[8,16,2,2,8,128]{5,4,3,2,1,0:T(8,128)} %bitcast.5, bf16[2,256,256]{2,1,0:T(8,128)(2,1)} %constant.11.clone.table, f32[512,512]{1,0:T(8,128)} %get-tuple-element.7.local_in), custom_call_target="tpu_custom_call" | custom-call | flops 1000000000 | bytes 8388608 | tf_op jit(solution)/shard_map/from_levels/pallas_call | solution.py:445

commit v2 on v1

--- a/solution.py
+++ b/solution.py
@@ -13,10 +13,11 @@
 PEERS = 16
 LEVELS = NZ // PEERS
 ROWS = NY // PEERS
-PAIRS = 4
-CHUNKS = 8
-AHEAD = 3
-VMEM = 67_043_328
+CHUNKS = 2 * MEMBERS
+AHEAD = 4
+PLANES = (0, 1, 2, 3, 7, 6, 4, 5)
+LEAD = (1, 0, 0, 0, 0, 0, 0, 0)
+VMEM = 67_043_328 - (3 << 20) - (256 << 10)
 F32, BF16 = jnp.float32, jnp.bfloat16
 MESH = pl.DeviceIdType.MESH
 NT = (((1,), (1,)), ((), ()))
@@ -41,13 +42,13 @@
 
 @functools.cache
 def y_table():
-    rows = np.meshgrid(np.arange(16), np.arange(2), np.arange(2), np.arange(2), np.arange(4), indexing="ij")
-    peer, out_part, low, out_member, out_level = (a.reshape(-1)[:, None] for a in rows)
-    columns = np.meshgrid(np.arange(2), np.arange(2), np.arange(32), np.arange(4), indexing="ij")
-    part, member, cell, level = (a.reshape(-1)[None, :] for a in columns)
+    rows = np.meshgrid(np.arange(16), np.arange(2), np.arange(2), np.arange(4), indexing="ij")
+    peer, out_part, low, out_level = (a.reshape(-1)[:, None] for a in rows)
+    columns = np.meshgrid(np.arange(2), np.arange(32), np.arange(4), indexing="ij")
+    part, cell, level = (a.reshape(-1)[None, :] for a in columns)
     angle = 2 * np.pi * (cell * (peer * 2 + low) % 32) / 32
     cross = np.where(out_part == 0, np.sin(angle), -np.sin(angle))
-    table = np.where(out_part == part, np.cos(angle), cross) * (member == out_member) * (level == out_level)
+    table = np.where(out_part == part, np.cos(angle), cross) * (level == out_level)
     return halves(table.astype(np.float32))
 
 
@@ -62,12 +63,12 @@
 @functools.cache
 def z_table():
     rows = np.meshgrid(np.arange(16), np.arange(2), np.arange(2), np.arange(4), indexing="ij")
-    peer, part, member, level = (a.reshape(-1)[:, None] for a in rows)
+    peer, part, low, level = (a.reshape(-1)[:, None] for a in rows)
     columns = np.meshgrid(np.arange(2), np.arange(2), np.arange(64), indexing="ij")
-    out_part, out_member, kz = (a.reshape(-1)[None, :] for a in columns)
+    out_part, out_low, kz = (a.reshape(-1)[None, :] for a in columns)
     angle = 2 * np.pi * ((4 * peer + level) * kz % NZ) / NZ
     cross = np.where(out_part == 0, np.sin(angle), -np.sin(angle))
-    table = np.where(out_part == part, np.cos(angle), cross) * (member == out_member)
+    table = np.where(out_part == part, np.cos(angle), cross) * (low == out_low)
     return halves(table.astype(np.float32))
 
 
@@ -132,12 +133,12 @@
 
 
 def exchange_kernel(
-    field, modes_in, x_tab, y_tab, y_twid,
-    levels_out, local_out,
-    cells, modes, x_t, y_t, tw, cells_parts, lines, blocks, y_parts, waves,
-    coef_one, coef_mine, coef_col, coef_row, coef_sum, coef_all, local_buf,
-    load_sem, row_send, row_recv, col_send, col_recv, own_sem,
-    small_send, small_recv, local_sem,
+    field, modes_in, x_tab, y_tab, y_twid, z_tab,
+    levels_out, local_out, z_t,
+    cells, modes, x_t, y_t, tw, cells_parts, lines, blocks, y_parts, waves, phases, chosen,
+    coef_one, coef_mine, coef_col, coef_row, coef_sum, coef_all,
+    load_sem, row_send, row_recv, col_send, col_recv,
+    small_send, small_recv,
 ):
     row, col = lax.axis_index("row"), lax.axis_index("col")
     z_at, y_lo = lax.rem(row, 8), row // 8
@@ -157,13 +158,12 @@
 
     pieces = [(x_tab, x_t)] + [(field.at[:, pl.ds(128 * t, 128)], cells.at[t]) for t in range(NX // 128)]
     first_pieces = len(pieces)
-    pieces += [(modes_in, modes), (y_twid, tw), (y_tab, y_t)]
+    pieces += [(modes_in, modes), (y_twid, tw), (y_tab, y_t), (z_tab, z_t)]
     loads = [pltpu.make_async_copy(source, target, load_sem.at[i]) for i, (source, target) in enumerate(pieces)]
     for each in loads:
         each.start()
 
-    def row_copy(chunk, k):
-        peer = row_peer(k)
+    def row_copy(chunk, peer):
         return pltpu.make_async_remote_copy(
             src_ref=lines.at[chunk, peer], dst_ref=blocks.at[chunk, row],
             send_sem=row_send.at[chunk], recv_sem=row_recv.at[chunk],
@@ -178,36 +178,51 @@
             device_id={"col": peer}, device_id_type=MESH,
         )
 
-    def own_copy(chunk):
-        return pltpu.make_async_copy(waves.at[chunk, col], levels_out.at[chunk, col], own_sem.at[chunk])
-
     def wait_bytes(ref, sem):
         pltpu.make_async_copy(ref, ref, sem).wait()
 
-    def send_rows(chunk):
-        @pl.loop(1, PEERS)
-        def _(k):
-            row_copy(chunk, k).start()
+    def send_rows(slot):
+        for plane, lead in zip(PLANES, LEAD):
+            chunk = slot + lead
+            there = jnp.logical_and(chunk >= 0, chunk < CHUNKS)
+            for peer in (plane, 8 + plane):
+
+                @pl.when(jnp.logical_and(there, peer != row))
+                def _(chunk=chunk, peer=peer):
+                    row_copy(chunk, peer).start()
 
     for each in loads[:first_pieces]:
         each.wait()
-    for pair in range(PAIRS):
-        for i in range(2):
-            for t in range(NX // 128):
-                high, low = split(cells[t, pl.ds(2 * pair + i, ROWS * LEVELS, stride=MEMBERS), :])
-                at = (pl.ds(i * 128, 128), pl.ds(t * 128, 128))
-                cells_parts[(0, *at)], cells_parts[(1, *at)] = high, low
+    def x_transform(member):
+        for t in range(NX // 128):
+            high, low = split(cells[t, pl.ds(member, ROWS * LEVELS, stride=MEMBERS), :])
+            lanes = pl.ds(t * 128, 128)
+            cells_parts[pl.ds(0, 128), lanes], cells_parts[pl.ds(128, 128), lanes] = high, low
         for half in range(2):
-            chunk = pair * 2 + half
+            chunk = member * 2 + half
             table = pl.ds(half * 256, 256)
-            high, low = cells_parts[0], cells_parts[1]
-            value = dot(x_t[0, table], high, NT) + dot(x_t[0, table], low, NT) + dot(x_t[1, table], high, NT)
-            lines[chunk] = value.reshape(PEERS, 16, 256)
+            both = dot(x_t[0, table], cells_parts[...], NT)
+            value = both[:, :128] + both[:, 128:] + dot(x_t[1, table], cells_parts[pl.ds(0, 128)], NT)
+            lines[chunk] = value.reshape(PEERS, 16, 128)
             blocks[chunk, row] = lines[chunk, row]
-            if chunk == 0:
-                pl.semaphore_wait(barrier, 2 * (PEERS - 1))
-            if chunk < AHEAD:
-                send_rows(chunk)
+
+    x_transform(0)
+    pl.semaphore_wait(barrier, 2 * (PEERS - 1))
+    for slot in range(-max(LEAD), 1):
+        send_rows(slot)
+
+    @pl.loop(1, MEMBERS)
+    def _(member):
+        x_transform(member)
+
+        @pl.when(member <= AHEAD // 2)
+        def _():
+            send_rows(2 * member - 1)
+
+        @pl.when(member < AHEAD // 2)
+        def _():
+            send_rows(2 * member)
+
     for each in loads[first_pieces:]:
         each.wait()
 
@@ -236,25 +251,24 @@
     steps = down(mode_row(1)) * cell + down(mode_row(2)) * level * float(NY // NZ)
     cos = cosine_of_turns(steps, float(NY))
     sin = cosine_of_turns(steps - 128.0, float(NY))
-    cos, sin = jnp.concatenate([cos, cos], axis=1), jnp.concatenate([sin, sin], axis=1)
-    lane_member = lax.broadcasted_iota(jnp.int32, (8, 256), 1) // 128
-    member = lax.broadcasted_iota(jnp.int32, (8, 256), 0)
-    coef_re = jnp.zeros((8, MODES), F32)
-    coef_im = jnp.zeros((8, MODES), F32)
-    for pair in range(PAIRS):
-        gather_member = (lane_member + 2 * pair == member).astype(F32).astype(BF16)
-        high, low = split(lines[2 * pair : 2 * pair + 2].reshape(512, 256))
-        at_modes = dot(choose, high, NN) + dot(choose, low, NN)
+    phases[0], phases[1] = cos, sin
+    chosen[...] = choose
+    own_member = lax.broadcasted_iota(jnp.int32, (8, 128), 0)
+
+    def add_member(member, coef):
+        here = (own_member == member).astype(F32).astype(BF16)
+        high, low = split(lines[pl.ds(2 * member, 2)].reshape(512, 128))
+        both = dot(chosen[...], jnp.concatenate([high, low], axis=1), NN)
+        at_modes = both[:, :128] + both[:, 128:]
         re, im = at_modes[:MODES], at_modes[MODES:]
-        sums = []
-        for value in (re * cos + im * sin, im * cos - re * sin):
-            high, low = split(value)
-            sums.append(dot(gather_member, high, NT) + dot(gather_member, low, NT))
-        coef_re += sums[0]
-        coef_im += sums[1]
-    for t in range(2):
-        coef_one[t] = coef_re[:, 128 * t : 128 * t + 128]
-        coef_one[2 + t] = coef_im[:, 128 * t : 128 * t + 128]
+        cos, sin = phases[0], phases[1]
+        value = jnp.concatenate([re * cos + im * sin, im * cos - re * sin], axis=0)
+        high, low = split(value)
+        return coef + dot(here, high, NT) + dot(here, low, NT)
+
+    coef = lax.fori_loop(0, MEMBERS, add_member, jnp.zeros((8, 2 * MODES), F32))
+    for t in range(4):
+        coef_one[t] = coef[:, 128 * t : 128 * t + 128]
 
     def tile_copy(k):
         peer = col_peer(k)
@@ -320,52 +334,43 @@
             for i in range(2):
                 at = slice(i * MODES, (i + 1) * MODES)
                 cov = dot(a_high[at], b_high, NN) + dot(a_high[at], b_low, NN) + dot(a_low[at], b_high, NN)
-                local_buf[at, :MODES] = cov[:, :MODES] * taper
-                local_buf[at, MODES:] = cov[:, MODES:] * taper
-            pltpu.make_async_copy(local_buf, local_out, local_sem).start()
+                local_out[at, :MODES] = cov[:, :MODES] * taper
+                local_out[at, MODES:] = cov[:, MODES:] * taper
 
     @pl.loop(0, CHUNKS)
     def _(chunk):
-        @pl.when(chunk + AHEAD < CHUNKS)
-        def _():
-            send_rows(chunk + AHEAD)
+        send_rows(chunk + AHEAD)
 
         wait_bytes(blocks.at[chunk, pl.ds(0, PEERS - 1)], row_recv.at[chunk])
-        for t in range(2):
-            lanes = pl.ds(t * 128, 128)
-            values = [(blocks[chunk, i, 0:8, lanes], blocks[chunk, i, 8:16, lanes]) for i in range(16)]
-            out = transform16(values)
-            for pair in range(8):
-                parts = []
-                for k1 in (2 * pair, 2 * pair + 1):
-                    re, im = out[k1]
-                    if k1 > 0:
-                        c = tw[2 * k1 : 2 * k1 + 1, :]
-                        s = tw[2 * k1 + 1 : 2 * k1 + 2, :]
-                        re, im = re * c + im * s, im * c - re * s
-                    parts.append((re, im))
-                for part in range(2):
-                    value = jnp.concatenate([parts[0][part], parts[1][part]], axis=0)
-                    high, low = split(value)
-                    at = pl.ds(part * 256 + t * 128, 128)
-                    y_parts[pl.ds(16 * pair, 16), at] = high
-                    y_parts[pl.ds(128 + 16 * pair, 16), at] = low
+        out = transform16([(blocks[chunk, i, 0:8, :], blocks[chunk, i, 8:16, :]) for i in range(16)])
+        for pair in range(8):
+            parts = []
+            for k1 in (2 * pair, 2 * pair + 1):
+                re, im = out[k1]
+                if k1 > 0:
+                    c = tw[2 * k1 : 2 * k1 + 1, :]
+                    s = tw[2 * k1 + 1 : 2 * k1 + 2, :]
+                    re, im = re * c + im * s, im * c - re * s
+                parts.append((re, im))
+            for part in range(2):
+                high, low = split(jnp.concatenate([parts[0][part], parts[1][part]], axis=0))
+                at = pl.ds(part * 128, 128)
+                y_parts[pl.ds(16 * pair, 16), at] = high
+                y_parts[pl.ds(128 + 16 * pair, 16), at] = low
         both = dot(y_t[0], y_parts[...], NT)
         value = both[:, :128] + both[:, 128:] + dot(y_t[1], y_parts[pl.ds(0, 128)], NT)
-        waves[chunk] = value.reshape(PEERS, 32, 128)
-
-        @pl.loop(1, PEERS)
-        def _(k):
+        waves[chunk] = value.reshape(PEERS, 16, 128)
+
+        for k in range(1, PEERS):
             col_copy(chunk, k).start()
 
-        own_copy(chunk).start()
-
-        for step, at in enumerate((1, 3, 5)):
+        levels_out[chunk, col] = waves[chunk, col]
+
+        for step, at in enumerate((2, 6, 10)):
             @pl.when(chunk == at)
             def _(step=step):
                 small_step(step)
 
-    pltpu.make_async_copy(local_buf, local_out, local_sem).wait()
     wait_bytes(coef_col.at[pl.ds(0, PEERS - 1)], small_send.at[0])
     wait_bytes(coef_row.at[pl.ds(0, PEERS - 1)], small_send.at[1])
     wait_bytes(coef_all.at[pl.ds(0, 3)], small_send.at[2])
@@ -374,7 +379,6 @@
     def _(chunk):
         wait_bytes(lines.at[chunk, pl.ds(0, PEERS - 1)], row_send.at[chunk])
         wait_bytes(waves.at[chunk, pl.ds(0, PEERS - 1)], col_send.at[chunk])
-        own_copy(chunk).wait()
         wait_bytes(levels_out.at[chunk, pl.ds(0, PEERS - 1)], col_recv.at[chunk])
 
 
@@ -384,91 +388,93 @@
     return pl.pallas_call(
         exchange_kernel,
         out_shape=(
-            jax.ShapeDtypeStruct((CHUNKS, PEERS, 32, 128), F32),
-            jax.ShapeDtypeStruct((2 * MODES, 2 * MODES), F32),
+            pltpu.VMEM((CHUNKS, PEERS, 16, 128), F32),
+            pltpu.VMEM((2 * MODES, 2 * MODES), F32),
+            pltpu.VMEM((2, 256, 256), BF16),
         ),
-        in_specs=[any_space] * 5,
-        out_specs=(any_space, any_space),
+        in_specs=[any_space] * 6,
+        out_specs=(pl.BlockSpec(memory_space=pltpu.VMEM),) * 3,
         scratch_shapes=[
             pltpu.VMEM((NX // 128, ROWS * LEVELS * MEMBERS, 128), F32),
             pltpu.VMEM((3, MODES), jnp.int32),
             pltpu.VMEM((2, 512, 512), BF16),
-            pltpu.VMEM((2, 512, 512), BF16),
+            pltpu.VMEM((2, 256, 256), BF16),
             pltpu.VMEM((32, 128), F32),
-            pltpu.VMEM((2, 256, NX), BF16),
-            pltpu.VMEM((CHUNKS, PEERS, 16, 256), F32),
-            pltpu.VMEM((CHUNKS, PEERS, 16, 256), F32),
-            pltpu.VMEM((256, 512), BF16),
-            pltpu.VMEM((CHUNKS, PEERS, 32, 128), F32),
+            pltpu.VMEM((256, NX), BF16),
+            pltpu.VMEM((CHUNKS, PEERS, 16, 128), F32),
+            pltpu.VMEM((CHUNKS, PEERS, 16, 128), F32),
+            pltpu.VMEM((256, 256), BF16),
+            pltpu.VMEM((CHUNKS, PEERS, 16, 128), F32),
+            pltpu.VMEM((2, MODES, 128), F32),
+            pltpu.VMEM((512, 512), BF16),
             pltpu.VMEM((4, 8, 128), F32),
             pltpu.VMEM((8, 128), F32),
             pltpu.VMEM((PEERS, 8, 128), F32),
             pltpu.VMEM((PEERS, 8, 128), F32),
             pltpu.VMEM((8, 128), F32),
             pltpu.VMEM((4, 8, 128), F32),
-            pltpu.VMEM((512, 512), F32),
-            dma((8,)),
-            dma((CHUNKS,)),
+            dma((9,)),
             dma((CHUNKS,)),
             dma((CHUNKS,)),
             dma((CHUNKS,)),
             dma((CHUNKS,)),
             dma((3,)),
             dma((3,)),
-            dma,
         ],
         compiler_params=pltpu.CompilerParams(collective_id=0, has_side_effects=True, vmem_limit_bytes=VMEM),
         cost_estimate=pl.CostEstimate(flops=10**10, bytes_accessed=8 << 20, transcendentals=0),
         name="exchange",
-    )(field.reshape(-1, NX), modes, x_table(), y_table(), y_twiddle())
-
-
-def levels_kernel(levels, table, local_in, spectrum, local, rows):
-    for half in range(2):
-        for low_k in range(2):
-            value = levels[half, :, :, low_k].reshape(256, 128).T
-            high, low = split(value)
+    )(field.reshape(-1, NX), modes, x_table(), y_table(), y_twiddle(), z_table())
+
+
+def levels_kernel(levels, table, local_in, spectrum, local, rows, ready, out_sem, local_sem):
+    local_copy = pltpu.make_async_copy(local_in, local, local_sem)
+    local_copy.start()
+    copies = []
+    for member in range(MEMBERS):
+        for half in range(2):
+            high, low = split(levels[2 * member + half].reshape(256, 128).T)
             out = dot(high, table[0], NN) + dot(high, table[1], NN) + dot(low, table[0], NN)
             for k1 in range(16):
                 for part in range(2):
-                    at = (low_k * 16 + k1) * 32 + 16 * half + part
+                    at = member * 512 + k1 * 32 + 16 * half + part
                     rows[pl.ds(at, 8, stride=2), :] = out[8 * k1 : 8 * k1 + 8, 128 * part : 128 * part + 128]
-    value = rows[...].reshape(NY // PEERS, 32, 128)
-    for member in range(2):
-        spectrum[:, member] = value[:, :, member * NZ : (member + 1) * NZ]
-    local[...] = local_in[...]
-
-
-def from_levels(levels, local):
-    levels = levels.reshape(CHUNKS, PEERS, 2, 2, 8, 128)
-    block = 2 * MODES // PAIRS
+        value = rows[pl.ds(member * 512, 512), :].reshape(16, 32, 128)
+        for low_k in range(2):
+            ready[pl.ds(low_k * 16, 16), member] = value[:, :, low_k * NZ : (low_k + 1) * NZ]
+        copies.append(pltpu.make_async_copy(ready.at[:, member], spectrum.at[:, member], out_sem.at[member]))
+        copies[-1].start()
+    for copy in copies:
+        copy.wait()
+    local_copy.wait()
+
+
+def from_levels(levels, local, table):
+    here = pl.BlockSpec(memory_space=pltpu.VMEM)
+    any_space = pl.BlockSpec(memory_space=pl.ANY)
     spectrum, local = pl.pallas_call(
         levels_kernel,
-        grid=(PAIRS,),
         out_shape=(
             jax.ShapeDtypeStruct((NY // PEERS, MEMBERS, 32, NZ), F32),
             jax.ShapeDtypeStruct((2 * MODES, 2 * MODES), F32),
         ),
-        in_specs=[
-            pl.BlockSpec((2, PEERS, 2, 2, 8, 128), lambda pair: (pair, 0, 0, 0, 0, 0)),
-            pl.BlockSpec((2, 256, 256), lambda pair: (0, 0, 0)),
-            pl.BlockSpec((block, 2 * MODES), lambda pair: (pair, 0)),
+        in_specs=[here] * 3,
+        out_specs=(any_space, any_space),
+        scratch_shapes=[
+            pltpu.VMEM((MEMBERS * 512, 128), F32),
+            pltpu.VMEM((NY // PEERS, MEMBERS, 32, NZ), F32),
+            pltpu.SemaphoreType.DMA((MEMBERS,)),
+            pltpu.SemaphoreType.DMA,
         ],
-        out_specs=(
-            pl.BlockSpec((NY // PEERS, 2, 32, NZ), lambda pair: (0, pair, 0, 0)),
-            pl.BlockSpec((block, 2 * MODES), lambda pair: (pair, 0)),
-        ),
-        scratch_shapes=[pltpu.VMEM((NY // PEERS * 32, 128), F32)],
         compiler_params=pltpu.CompilerParams(vmem_limit_bytes=VMEM),
         cost_estimate=pl.CostEstimate(flops=10**9, bytes_accessed=8 << 20, transcendentals=0),
         name="from_levels",
-    )(levels, z_table(), local)
+    )(*(pltpu.with_memory_space_constraint(each, pltpu.VMEM) for each in (levels, table, local)))
     return jnp.transpose(spectrum, (3, 0, 1, 2)), local
 
 
 def per_device(field, modes):
-    levels, local = exchange(field, modes)
-    return from_levels(levels, local)
+    return from_levels(*exchange(field, modes))
 
 
 def solution(mesh):

time: 74.4 us -> 70.2 us (0.944)
  Pallas kernels: 73.6 us -> 68.8 us
    pallas_call x2, Pallas kernels: 73.6 us -> 68.8 us  [the longest x1 66 us: exchange(): pl.pallas_call(exchange_kernel, out_shape=(pltpu.VMEM((CHUNKS, PEERS, 16,...]
where the time goes in v2:
time: 70.2 us; the launch traced here: 69.5 us
  Pallas kernels  68.8 us (98%)
    pallas_call x1, Pallas kernels, exchange(): pl.pallas_call(exchange_kernel, out_shape=(pltpu.VMEM((CHUNKS, PEERS, 16,...  66 us
    pallas_call x1, Pallas kernels, from_levels(): pl.pallas_call(levels_kernel, out_shape=(jax.ShapeDtypeStruct((NY // PEER...  2.88 us

profile of v2, /device:TPU:1, one launch (start us, length us, event | category | flops | bytes accessed | tf_op | source)
XLA Modules:
  0.0 69.5 jit_solution(3113085888269817930)
XLA Ops:
  0.6 66.0 %exchange.1 = (f32[16,16,16,128]{3,2,1,0:T(8,128)S(1)}, f32[512,512]{1,0:T(8,128)S(1)}, bf16[2,256,256]{2,1,0:T(8,128)(2,1)S(1)}) custom-call(f32[1024,512]{1,0:T(8,128)} %bitcast.2, s32[3,256]{1,0:T(4,128)} %modes_in.1, bf16[2,512,512]{2,1,0:T(8,128)(2,1)} %constant.8.clone.x_tab, bf16[2,256,256]{2,1,0:T(8,128)(2,1)} %constant.9.clone.y_tab, ...), custom_call_target="tpu_custom_call" | custom-call | flops 10000000000 | bytes 8388608 | tf_op jit(solution)/shard_map/exchange/pallas_call | solution.py:388
  66.6 2.9 %from_levels.1 = (f32[32,8,32,64]{3,2,1,0:T(8,128)}, f32[512,512]{1,0:T(8,128)}) custom-call(f32[16,16,16,128]{3,2,1,0:T(8,128)S(1)} %get-tuple-element.7.levels, bf16[2,256,256]{2,1,0:T(8,128)(2,1)S(1)} %get-tuple-element.8.table, f32[512,512]{1,0:T(8,128)S(1)} %get-tuple-element.9.local_in), custom_call_target="tpu_custom_call" | custom-call | flops 1000000000 | bytes 8388608 | tf_op jit(solution)/shard_map/from_levels/pallas_call | solution.py:455

commit v3 on v2

--- a/solution.py
+++ b/solution.py
@@ -15,9 +15,10 @@
 ROWS = NY // PEERS
 CHUNKS = 2 * MEMBERS
 AHEAD = 4
+DONE = MEMBERS - 1
 PLANES = (0, 1, 2, 3, 7, 6, 4, 5)
 LEAD = (1, 0, 0, 0, 0, 0, 0, 0)
-VMEM = 67_043_328 - (3 << 20) - (256 << 10)
+VMEM = 67_043_328 - (7 << 20) - (256 << 10)
 F32, BF16 = jnp.float32, jnp.bfloat16
 MESH = pl.DeviceIdType.MESH
 NT = (((1,), (1,)), ((), ()))
@@ -132,10 +133,23 @@
     return -(poly * s)
 
 
+def z_transform(levels, table, rows, ready, member):
+    for half in range(2):
+        high, low = split(levels[2 * member + half].reshape(256, 128).T)
+        out = dot(high, table[0], NN) + dot(high, table[1], NN) + dot(low, table[0], NN)
+        for k1 in range(16):
+            for part in range(2):
+                at = k1 * 32 + 16 * half + part
+                rows[pl.ds(at, 8, stride=2), :] = out[8 * k1 : 8 * k1 + 8, 128 * part : 128 * part + 128]
+    value = rows[...].reshape(16, 32, 128)
+    for low_k in range(2):
+        ready[pl.ds(low_k * 16, 16)] = value[:, :, low_k * NZ : (low_k + 1) * NZ]
+
+
 def exchange_kernel(
     field, modes_in, x_tab, y_tab, y_twid, z_tab,
-    levels_out, local_out, z_t,
-    cells, modes, x_t, y_t, tw, cells_parts, lines, blocks, y_parts, waves, phases, chosen,
+    levels_out, local_out, z_t, ready,
+    cells, modes, x_t, y_t, tw, cells_parts, lines, blocks, y_parts, waves, phases, chosen, z_rows,
     coef_one, coef_mine, coef_col, coef_row, coef_sum, coef_all,
     load_sem, row_send, row_recv, col_send, col_recv,
     small_send, small_recv,
@@ -146,15 +160,18 @@
     def row_peer(k):
         return lax.rem(z_at + k, 8) + 8 * lax.rem(y_lo + k // 8, 2)
 
+    x_at, y_hi, core = col // 4, lax.rem(col // 2, 2), lax.rem(col, 2)
+
     def col_peer(k):
-        return lax.rem(col + k, PEERS)
+        x_step, y_step, core_step = (2, 1, 3, 0)[(k - 1) // 4], 1 - ((k - 1) // 2) % 2, k % 2
+        return lax.rem(x_at + x_step, 4) * 4 + lax.rem(y_hi + y_step, 2) * 2 + lax.rem(core + core_step, 2)
 
     barrier = pltpu.get_barrier_semaphore()
 
     @pl.loop(1, PEERS)
     def _(k):
         pl.semaphore_signal(barrier, inc=1, device_id={"row": row_peer(k)}, device_id_type=MESH)
-        pl.semaphore_signal(barrier, inc=1, device_id={"col": col_peer(k)}, device_id_type=MESH)
+        pl.semaphore_signal(barrier, inc=1, device_id={"col": lax.rem(col + k, PEERS)}, device_id_type=MESH)
 
     pieces = [(x_tab, x_t)] + [(field.at[:, pl.ds(128 * t, 128)], cells.at[t]) for t in range(NX // 128)]
     first_pieces = len(pieces)
@@ -268,12 +285,13 @@
 
     coef = lax.fori_loop(0, MEMBERS, add_member, jnp.zeros((8, 2 * MODES), F32))
     for t in range(4):
-        coef_one[t] = coef[:, 128 * t : 128 * t + 128]
-
-    def tile_copy(k):
+        for pair in range(4):
+            coef_one[4 * t + pair] = coef[2 * pair : 2 * pair + 2, 128 * t : 128 * t + 128]
+
+    def piece_copy(k):
         peer = col_peer(k)
         return pltpu.make_async_remote_copy(
-            src_ref=coef_one.at[lax.rem(peer, 4)], dst_ref=coef_col.at[col],
+            src_ref=coef_one.at[peer], dst_ref=coef_col.at[col],
             send_sem=small_send.at[0], recv_sem=small_recv.at[0], device_id={"col": peer}, device_id_type=MESH,
         )
 
@@ -284,19 +302,17 @@
         )
 
     def share_copy(k):
-        peer = (col // 4) * 4 + lax.rem(col + k, 4)
         return pltpu.make_async_remote_copy(
-            src_ref=coef_sum, dst_ref=coef_all.at[lax.rem(col, 4)],
-            send_sem=small_send.at[2], recv_sem=small_recv.at[2], device_id={"col": peer}, device_id_type=MESH,
+            src_ref=coef_sum, dst_ref=coef_all.at[col],
+            send_sem=small_send.at[2], recv_sem=small_recv.at[2], device_id={"col": col_peer(k)}, device_id_type=MESH,
         )
 
-    def start_all(copy, count):
-        @pl.loop(1, count)
-        def _(k):
+    def start_all(copy):
+        for k in range(1, PEERS):
             copy(k).start()
 
-    coef_col[col] = coef_one[lax.rem(col, 4)]
-    start_all(tile_copy, PEERS)
+    coef_col[col] = coef_one[col]
+    start_all(piece_copy)
 
     def small_step(step):
         if step == 0:
@@ -306,18 +322,19 @@
                 total = total + coef_col[i]
             coef_mine[...] = total
             coef_row[row] = total
-            start_all(sum_copy, PEERS)
+            start_all(sum_copy)
         elif step == 1:
             wait_bytes(coef_row.at[pl.ds(0, PEERS - 1)], small_recv.at[1])
             total = coef_row[0]
             for i in range(1, PEERS):
                 total = total + coef_row[i]
             coef_sum[...] = total
-            coef_all[lax.rem(col, 4)] = total
-            start_all(share_copy, 4)
+            coef_all[col] = total
+            start_all(share_copy)
         else:
-            wait_bytes(coef_all.at[pl.ds(0, 3)], small_recv.at[2])
-            coef = jnp.concatenate([coef_all[i] for i in range(4)], axis=1)
+            wait_bytes(coef_all.at[pl.ds(0, PEERS - 1)], small_recv.at[2])
+            tiles = [jnp.concatenate([coef_all[4 * t + pair] for pair in range(4)], axis=0) for t in range(4)]
+            coef = jnp.concatenate(tiles, axis=1)
             anomaly = coef - jnp.mean(coef, axis=0, keepdims=True)
             turned = anomaly.T
             a_high, a_low = split(turned)
@@ -366,20 +383,32 @@
 
         levels_out[chunk, col] = waves[chunk, col]
 
-        for step, at in enumerate((2, 6, 10)):
+        for step, at in enumerate((4, 9)):
             @pl.when(chunk == at)
             def _(step=step):
                 small_step(step)
 
+    small_step(2)
+
+    def wait_levels(member):
+        for chunk in (2 * member, 2 * member + 1):
+            wait_bytes(levels_out.at[chunk, pl.ds(0, PEERS - 1)], col_recv.at[chunk])
+
+    @pl.loop(0, DONE)
+    def _(member):
+        wait_levels(member)
+        z_transform(levels_out, z_t, z_rows, ready.at[member], member)
+
+    for member in range(DONE, MEMBERS):
+        wait_levels(member)
     wait_bytes(coef_col.at[pl.ds(0, PEERS - 1)], small_send.at[0])
     wait_bytes(coef_row.at[pl.ds(0, PEERS - 1)], small_send.at[1])
-    wait_bytes(coef_all.at[pl.ds(0, 3)], small_send.at[2])
+    wait_bytes(coef_all.at[pl.ds(0, PEERS - 1)], small_send.at[2])
 
     @pl.loop(0, CHUNKS)
     def _(chunk):
         wait_bytes(lines.at[chunk, pl.ds(0, PEERS - 1)], row_send.at[chunk])
         wait_bytes(waves.at[chunk, pl.ds(0, PEERS - 1)], col_send.at[chunk])
-        wait_bytes(levels_out.at[chunk, pl.ds(0, PEERS - 1)], col_recv.at[chunk])
 
 
 def exchange(field, modes):
@@ -391,9 +420,10 @@
             pltpu.VMEM((CHUNKS, PEERS, 16, 128), F32),
             pltpu.VMEM((2 * MODES, 2 * MODES), F32),
             pltpu.VMEM((2, 256, 256), BF16),
+            pltpu.VMEM((MEMBERS, NY // PEERS, 32, NZ), F32),
         ),
         in_specs=[any_space] * 6,
-        out_specs=(pl.BlockSpec(memory_space=pltpu.VMEM),) * 3,
+        out_specs=(pl.BlockSpec(memory_space=pltpu.VMEM),) * 4,
         scratch_shapes=[
             pltpu.VMEM((NX // 128, ROWS * LEVELS * MEMBERS, 128), F32),
             pltpu.VMEM((3, MODES), jnp.int32),
@@ -407,12 +437,13 @@
             pltpu.VMEM((CHUNKS, PEERS, 16, 128), F32),
             pltpu.VMEM((2, MODES, 128), F32),
             pltpu.VMEM((512, 512), BF16),
-            pltpu.VMEM((4, 8, 128), F32),
-            pltpu.VMEM((8, 128), F32),
-            pltpu.VMEM((PEERS, 8, 128), F32),
-            pltpu.VMEM((PEERS, 8, 128), F32),
-            pltpu.VMEM((8, 128), F32),
-            pltpu.VMEM((4, 8, 128), F32),
+            pltpu.VMEM((512, 128), F32),
+            pltpu.VMEM((PEERS, 2, 128), F32),
+            pltpu.VMEM((2, 128), F32),
+            pltpu.VMEM((PEERS, 2, 128), F32),
+            pltpu.VMEM((PEERS, 2, 128), F32),
+            pltpu.VMEM((2, 128), F32),
+            pltpu.VMEM((PEERS, 2, 128), F32),
             dma((9,)),
             dma((CHUNKS,)),
             dma((CHUNKS,)),
@@ -427,29 +458,22 @@
     )(field.reshape(-1, NX), modes, x_table(), y_table(), y_twiddle(), z_table())
 
 
-def levels_kernel(levels, table, local_in, spectrum, local, rows, ready, out_sem, local_sem):
-    local_copy = pltpu.make_async_copy(local_in, local, local_sem)
-    local_copy.start()
-    copies = []
+def levels_kernel(levels, local_in, table, ready, spectrum, local, rows, last, out_sem, local_sem):
+    copies = [pltpu.make_async_copy(local_in, local, local_sem)]
     for member in range(MEMBERS):
-        for half in range(2):
-            high, low = split(levels[2 * member + half].reshape(256, 128).T)
-            out = dot(high, table[0], NN) + dot(high, table[1], NN) + dot(low, table[0], NN)
-            for k1 in range(16):
-                for part in range(2):
-                    at = member * 512 + k1 * 32 + 16 * half + part
-                    rows[pl.ds(at, 8, stride=2), :] = out[8 * k1 : 8 * k1 + 8, 128 * part : 128 * part + 128]
-        value = rows[pl.ds(member * 512, 512), :].reshape(16, 32, 128)
-        for low_k in range(2):
-            ready[pl.ds(low_k * 16, 16), member] = value[:, :, low_k * NZ : (low_k + 1) * NZ]
-        copies.append(pltpu.make_async_copy(ready.at[:, member], spectrum.at[:, member], out_sem.at[member]))
-        copies[-1].start()
+        source = ready.at[member] if member < DONE else last.at[member - DONE]
+        copies.append(pltpu.make_async_copy(source, spectrum.at[:, member], out_sem.at[member]))
+    for copy in copies[1 : DONE + 1]:
+        copy.start()
+    copies[0].start()
+    for member in range(DONE, MEMBERS):
+        z_transform(levels, table, rows, last.at[member - DONE], member)
+        copies[member + 1].start()
     for copy in copies:
         copy.wait()
-    local_copy.wait()
-
-
-def from_levels(levels, local, table):
+
+
+def from_levels(*parts):
     here = pl.BlockSpec(memory_space=pltpu.VMEM)
     any_space = pl.BlockSpec(memory_space=pl.ANY)
     spectrum, local = pl.pallas_call(
@@ -458,18 +482,18 @@
             jax.ShapeDtypeStruct((NY // PEERS, MEMBERS, 32, NZ), F32),
             jax.ShapeDtypeStruct((2 * MODES, 2 * MODES), F32),
         ),
-        in_specs=[here] * 3,
+        in_specs=[here] * 4,
         out_specs=(any_space, any_space),
         scratch_shapes=[
-            pltpu.VMEM((MEMBERS * 512, 128), F32),
-            pltpu.VMEM((NY // PEERS, MEMBERS, 32, NZ), F32),
+            pltpu.VMEM((512, 128), F32),
+            pltpu.VMEM((MEMBERS - DONE, NY // PEERS, 32, NZ), F32),
             pltpu.SemaphoreType.DMA((MEMBERS,)),
             pltpu.SemaphoreType.DMA,
         ],
         compiler_params=pltpu.CompilerParams(vmem_limit_bytes=VMEM),
         cost_estimate=pl.CostEstimate(flops=10**9, bytes_accessed=8 << 20, transcendentals=0),
         name="from_levels",
-    )(*(pltpu.with_memory_space_constraint(each, pltpu.VMEM) for each in (levels, table, local)))
+    )(*(pltpu.with_memory_space_constraint(each, pltpu.VMEM) for each in parts))
     return jnp.transpose(spectrum, (3, 0, 1, 2)), local
 
 

time: 70.2 us -> 67.1 us (0.956)
  Pallas kernels: 68.8 us -> 66.2 us
    pallas_call x1, Pallas kernels: 66 us -> 63.8 us  [exchange(): pl.pallas_call(exchange_kernel, out_shape=(pltpu.VMEM((CHUNKS, PEERS, 16,...]
where the time goes in v3:
time: 67.1 us; the launch traced here: 66.9 us
  Pallas kernels  66.2 us (99%)
    pallas_call x1, Pallas kernels, exchange(): pl.pallas_call(exchange_kernel, out_shape=(pltpu.VMEM((CHUNKS, PEERS, 16,...  63.8 us
    pallas_call x1, Pallas kernels, from_levels(): pl.pallas_call(levels_kernel, out_shape=(jax.ShapeDtypeStruct((NY // PEER...  2.43 us

profile of v3, /device:TPU:1, one launch (start us, length us, event | category | flops | bytes accessed | tf_op | source)
XLA Modules:
  0.0 66.9 jit_solution(11105557953759776403)
XLA Ops:
  0.6 63.8 %exchange.1 = (f32[16,16,16,128]{3,2,1,0:T(8,128)S(1)}, f32[512,512]{1,0:T(8,128)S(1)}, bf16[2,256,256]{2,1,0:T(8,128)(2,1)S(1)}, f32[8,32,32,64]{3,2,1,0:T(8,128)S(1)}) custom-call(f32[1024,512]{1,0:T(8,128)} %bitcast.3, s32[3,256]{1,0:T(4,128)} %modes_in.1, bf16[2,512,512]{2,1,0:T(8,128)(2,1)} %constant.8.clone.x_tab, ...), custom_call_target="tpu_custom_call" | custom-call | flops 10000000000 | bytes 8388608 | tf_op jit(solution)/shard_map/exchange/pallas_call | solution.py:417
  64.5 2.4 %from_levels.1 = (f32[32,8,32,64]{3,2,1,0:T(8,128)}, f32[512,512]{1,0:T(8,128)}) custom-call(f32[16,16,16,128]{3,2,1,0:T(8,128)S(1)} %get-tuple-element.8.levels, f32[512,512]{1,0:T(8,128)S(1)} %get-tuple-element.9.local_in, bf16[2,256,256]{2,1,0:T(8,128)(2,1)S(1)} %get-tuple-element.10.table, f32[8,32,32,64]{3,2,1,0:T(8,128)S(1)} %get-tuple-element.11.ready), custom_call_target="tpu_custom_call" | custom-call | flops 1000000000 | bytes 8388608 | tf_op jit(solution)/shard_map/from_levels/pallas_call | solution.py:479

commit v4 on v3

--- a/solution.py
+++ b/solution.py
@@ -17,7 +17,7 @@
 AHEAD = 4
 DONE = MEMBERS - 1
 PLANES = (0, 1, 2, 3, 7, 6, 4, 5)
-LEAD = (1, 0, 0, 0, 0, 0, 0, 0)
+LEAD = (2, 1, 1, 0, 0, 0, 0, 0)
 VMEM = 67_043_328 - (7 << 20) - (256 << 10)
 F32, BF16 = jnp.float32, jnp.bfloat16
 MESH = pl.DeviceIdType.MESH
@@ -168,10 +168,13 @@
 
     barrier = pltpu.get_barrier_semaphore()
 
-    @pl.loop(1, PEERS)
-    def _(k):
-        pl.semaphore_signal(barrier, inc=1, device_id={"row": row_peer(k)}, device_id_type=MESH)
-        pl.semaphore_signal(barrier, inc=1, device_id={"col": lax.rem(col + k, PEERS)}, device_id_type=MESH)
+    for z_step in (4, 3, 5, 2, 6, 1, 7, 0):
+        for y_step in (1, 0):
+            if z_step or y_step:
+                peer = lax.rem(z_at + z_step, 8) + 8 * lax.rem(y_lo + y_step, 2)
+                pl.semaphore_signal(barrier, inc=1, device_id={"row": peer}, device_id_type=MESH)
+    for k in range(1, PEERS):
+        pl.semaphore_signal(barrier, inc=1, device_id={"col": col_peer(k)}, device_id_type=MESH)
 
     pieces = [(x_tab, x_t)] + [(field.at[:, pl.ds(128 * t, 128)], cells.at[t]) for t in range(NX // 128)]
     first_pieces = len(pieces)
@@ -202,7 +205,7 @@
         for plane, lead in zip(PLANES, LEAD):
             chunk = slot + lead
             there = jnp.logical_and(chunk >= 0, chunk < CHUNKS)
-            for peer in (plane, 8 + plane):
+            for peer in (plane + 8 * (1 - y_lo), plane + 8 * y_lo):
 
                 @pl.when(jnp.logical_and(there, peer != row))
                 def _(chunk=chunk, peer=peer):
@@ -225,7 +228,7 @@
 
     x_transform(0)
     pl.semaphore_wait(barrier, 2 * (PEERS - 1))
-    for slot in range(-max(LEAD), 1):
+    for slot in (-2, -1):
         send_rows(slot)
 
     @pl.loop(1, MEMBERS)
@@ -234,11 +237,8 @@
 
         @pl.when(member <= AHEAD // 2)
         def _():
+            send_rows(2 * member - 2)
             send_rows(2 * member - 1)
-
-        @pl.when(member < AHEAD // 2)
-        def _():
-            send_rows(2 * member)
 
     for each in loads[first_pieces:]:
         each.wait()

time: 67.1 us -> 66.4 us (0.990)
  no operation moved by 1% of the time
where the time goes in v4:
time: 66.4 us; the launch traced here: 66.3 us
  Pallas kernels  65.7 us (99%)
    pallas_call x1, Pallas kernels, exchange(): pl.pallas_call(exchange_kernel, out_shape=(pltpu.VMEM((CHUNKS, PEERS, 16,...  63.3 us
    pallas_call x1, Pallas kernels, from_levels(): pl.pallas_call(levels_kernel, out_shape=(jax.ShapeDtypeStruct((NY // PEER...  2.43 us

profile of v4, /device:TPU:1, one launch (start us, length us, event | category | flops | bytes accessed | tf_op | source)
XLA Modules:
  0.0 66.3 jit_solution(15424472117572245525)
XLA Ops:
  0.6 63.3 %exchange.1 = (f32[16,16,16,128]{3,2,1,0:T(8,128)S(1)}, f32[512,512]{1,0:T(8,128)S(1)}, bf16[2,256,256]{2,1,0:T(8,128)(2,1)S(1)}, f32[8,32,32,64]{3,2,1,0:T(8,128)S(1)}) custom-call(f32[1024,512]{1,0:T(8,128)} %bitcast.3, s32[3,256]{1,0:T(4,128)} %modes_in.1, bf16[2,512,512]{2,1,0:T(8,128)(2,1)} %constant.8.clone.x_tab, ...), custom_call_target="tpu_custom_call" | custom-call | flops 10000000000 | bytes 8388608 | tf_op jit(solution)/shard_map/exchange/pallas_call | solution.py:417
  63.9 2.4 %from_levels.1 = (f32[32,8,32,64]{3,2,1,0:T(8,128)}, f32[512,512]{1,0:T(8,128)}) custom-call(f32[16,16,16,128]{3,2,1,0:T(8,128)S(1)} %get-tuple-element.8.levels, f32[512,512]{1,0:T(8,128)S(1)} %get-tuple-element.9.local_in, bf16[2,256,256]{2,1,0:T(8,128)(2,1)S(1)} %get-tuple-element.10.table, f32[8,32,32,64]{3,2,1,0:T(8,128)S(1)} %get-tuple-element.11.ready), custom_call_target="tpu_custom_call" | custom-call | flops 1000000000 | bytes 8388608 | tf_op jit(solution)/shard_map/from_levels/pallas_call | solution.py:479
